TPU v7x, 32 devices: a whole 2x2x4 slice. The times are simulated.
32 devices in a mesh: cell: 16 (over z, y, core), tm: 2 (over x).
Axes of the slice: x: 2, y: 2, z: 4, core: 2. Of those that a mesh axis runs over, the one named last changes fastest.
Arguments:
- anomalies: float32 [32768, 2048], P('cell', 'tm'), may hold values from -6 to 6
- start_basis: float32 [2048, 128], P('tm'), may hold values from -0.125 to 0.125
Outputs:
- patterns: float32 [32768, 128], P(('cell', 'tm'))
All inputs are finite; a program needn't handle non-finite values.
Results may differ from a plain program's by a relative error of at most 0.0003.
Values sent between devices are 32-bit elements; how exact they have to be, the bound alone decides.
A program may use at most 64 MiB of HBM per device.

v0:
```python
import jax
import jax.numpy as jnp
from jax import lax
from jax.sharding import PartitionSpec as P

ITERS = 2


def tall_product(left, right):
    return lax.dot_general(
        left,
        right,
        (((0,), (0,)), ((), ())),
        precision=lax.Precision.HIGHEST,
        preferred_element_type=jnp.float32,
    )


def orthonormal(gram, image):
    lower = jnp.linalg.cholesky(gram)
    return jax.scipy.linalg.solve_triangular(lower, image.T, lower=True).T


def on_device(anomalies, start_basis):
    full = lax.Precision.HIGHEST
    basis = start_basis
    for step in range(ITERS):
        current = basis
        local_terms = jnp.dot(
            anomalies, current, precision=full, preferred_element_type=jnp.float32
        )
        spatial = lax.psum(local_terms, "tm")
        partial_value = tall_product(anomalies, spatial)
        image = lax.psum(partial_value, "cell")
        gram = lax.psum(tall_product(image, image), "tm")
        basis = orthonormal(gram, image)
    return lax.psum_scatter(
        jnp.dot(anomalies, basis, precision=full, preferred_element_type=jnp.float32),
        "tm",
        scatter_dimension=0,
        tiled=True,
    )


def solution(mesh):
    in_specs = (P("cell", "tm"), P("tm", None))
    out_specs = P(("cell", "tm"), None)
    return jax.shard_map(
        on_device, mesh=mesh, in_specs=in_specs, out_specs=out_specs, check_vma=False
    )
```

profile of v0, /device:TPU:0, one launch (start us, length us, event | category | flops | bytes accessed | tf_op | source)
XLA Modules:
  0.0 454.8 jit_solution(14277269231684807077)
XLA Ops:
  6.5 1.0 copy-done
  7.6 9.8 %fusion.12 = f32[2048,128]{1,0:T(8,128)} fusion(f32[2048,1024]{1,0:T(8,128)} %param.5, f32[1024,128]{1,0:T(8,128)S(1)} %copy-done), kind=kOutput, calls=%fused_computation.25 | convolution fusion | flops 3221225472 | bytes 9961472 | tf_op jit(solution)/shard_map/dot_general | solution.py:29
  17.5 42.9 %all-reduce.7.cloned.1.call-done = f32[2048,128]{1,0:T(8,128)} async-done(((f32[2048,128]{1,0:T(8,128)}), f32[2048,128]{1,0:T(8,128)}) %all-reduce.7.cloned.1.call-update) | async-done | bytes 1048592 | tf_op jit(solution)/shard_map/psum | solution.py:32
  60.4 9.1 %convolution_bitcast_fusion.3 = f32[1024,128]{0,1:T(8,128)} fusion(f32[2048,128]{1,0:T(8,128)} %all-reduce.7.cloned.1.call-done, f32[2048,1024]{1,0:T(8,128)} %param.5), kind=kOutput, calls=%fused_computation.3 | convolution fusion | flops 3221225472 | bytes 9961472 | tf_op jit(solution)/shard_map/dot_general | solution.py:10
  69.7 90.8 %all-reduce.9.cloned.1.call-done = f32[1024,128]{0,1:T(8,128)} async-done(((f32[1024,128]{0,1:T(8,128)}), f32[1024,128]{0,1:T(8,128)}) %all-reduce.9.cloned.1.call-update) | async-done | bytes 524304 | tf_op jit(solution)/shard_map/psum | solution.py:34
  160.4 2.4 fusion.13
  163.1 21.3 %all-reduce.11.cloned.1.call-done = f32[128,128]{0,1:T(8,128)} async-done(((f32[128,128]{0,1:T(8,128)}), f32[128,128]{0,1:T(8,128)}) %all-reduce.11.cloned.1.call-update) | async-done | bytes 65552 | tf_op jit(solution)/shard_map/psum | solution.py:35
  184.4 0.9 copy.4
  186.2 11.7 %cholesky.44 = f32[128,128]{1,0:T(8,128)S(1)} custom-call(f32[128,128]{1,0:T(8,128)S(1)} %fusion.9), custom_call_target="Cholesky" | custom-call | tf_op jit(solution)/shard_map/jit(cholesky)/cholesky | solution.py:20
  199.3 9.8 %custom-call.6 = f32[1,128,128]{1,2,0:T(8,128)S(1)} custom-call(f32[1,128,128]{2,1,0:T(8,128)S(1)} %fusion.4), custom_call_target="InvertDiagBlocksLowerTriangular" | custom-call | tf_op jit(solution)/shard_map/jit(_solve_triangular)/triangular_solve | solution.py:21
  209.1 1.7 fusion.2
  210.8 12.0 %convolution_bitcast_fusion.1 = f32[2048,128]{0,1:T(8,128)} fusion(f32[128,1024]{1,0:T(8,128)S(1)} %fusion.2, f32[2048,1024]{1,0:T(8,128)} %param.5), kind=kOutput, calls=%fused_computation.1 | convolution fusion | flops 3221225472 | bytes 9961472 | tf_op jit(solution)/shard_map/dot_general | solution.py:29
  222.8 40.2 %all-reduce.13.cloned.1.call-done = f32[2048,128]{0,1:T(8,128)} async-done(((f32[2048,128]{0,1:T(8,128)}), f32[2048,128]{0,1:T(8,128)}) %all-reduce.13.cloned.1.call-update) | async-done | bytes 1048592 | tf_op jit(solution)/shard_map/psum | solution.py:32
  263.0 9.2 %convolution_bitcast_fusion.2 = f32[1024,128]{0,1:T(8,128)} fusion(f32[2048,128]{0,1:T(8,128)} %all-reduce.13.cloned.1.call-done, f32[2048,1024]{1,0:T(8,128)} %param.5), kind=kOutput, calls=%fused_computation.2 | convolution fusion | flops 3221225472 | bytes 9961472 | tf_op jit(solution)/shard_map/dot_general | solution.py:10
  272.3 90.8 %all-reduce.15.cloned.1.call-done = f32[1024,128]{0,1:T(8,128)} async-done(((f32[1024,128]{0,1:T(8,128)}), f32[1024,128]{0,1:T(8,128)}) %all-reduce.15.cloned.1.call-update) | async-done | bytes 524304 | tf_op jit(solution)/shard_map/psum | solution.py:34
  363.1 2.4 fusion.14
  365.8 21.3 %all-reduce.17.cloned.1.call-done = f32[128,128]{0,1:T(8,128)} async-done(((f32[128,128]{0,1:T(8,128)}), f32[128,128]{0,1:T(8,128)}) %all-reduce.17.cloned.1.call-update) | async-done | bytes 65552 | tf_op jit(solution)/shard_map/psum | solution.py:35
  387.1 0.9 copy.6
  388.9 11.7 %cholesky.55 = f32[128,128]{1,0:T(8,128)S(1)} custom-call(f32[128,128]{1,0:T(8,128)S(1)} %fusion.7), custom_call_target="Cholesky" | custom-call | tf_op jit(solution)/shard_map/jit(cholesky)/cholesky | solution.py:20
  401.9 9.8 %custom-call.7 = f32[1,128,128]{1,2,0:T(8,128)S(1)} custom-call(f32[1,128,128]{2,1,0:T(8,128)S(1)} %fusion.5), custom_call_target="InvertDiagBlocksLowerTriangular" | custom-call | tf_op jit(solution)/shard_map/jit(_solve_triangular)/triangular_solve | solution.py:21
  411.7 1.7 fusion
  413.4 11.9 %convolution_bitcast_fusion = f32[2048,128]{0,1:T(8,128)} fusion(f32[128,1024]{1,0:T(8,128)S(1)} %fusion, f32[2048,1024]{1,0:T(8,128)} %param.5), kind=kOutput, calls=%fused_computation | convolution fusion | flops 3221225472 | bytes 9961472 | tf_op jit(solution)/shard_map/dot_general | solution.py:38
  425.4 20.5 %reduce-scatter.2.cloned.1.call-done = f32[1024,128]{0,1:T(8,128)} async-done(((f32[2048,128]{0,1:T(8,128)}), f32[1024,128]{0,1:T(8,128)}) %reduce-scatter.2.cloned.1.call-update) | async-done | bytes 524304 | tf_op jit(solution)/shard_map/reduce_scatter | solution.py:37
  445.9 2.0 copy.7
  (23 shorter events, 5.2 us)
Async XLA Ops:
  6.5 1.0 copy-start
  6.5 53.9 %all-reduce.7.cloned.1.call-start = ((), (), s32[]{:S(2)}) async-start(), calls=%async_computation.1 | async-start | bytes 2097152 | tf_op jit(solution)/shard_map/psum | solution.py:32
  17.4 143.0 %all-reduce.9.cloned.1.call-start = ((), (), s32[]{:S(2)}) async-start(), calls=%async_computation.2 | async-start | bytes 1048576 | tf_op jit(solution)/shard_map/psum | solution.py:34
  69.6 114.8 %all-reduce.11.cloned.1.call-start = ((), (), s32[]{:S(2)}) async-start(), calls=%async_computation.3 | async-start | bytes 131072 | tf_op jit(solution)/shard_map/psum | solution.py:35
  162.9 100.2 %all-reduce.13.cloned.1.call-start = ((), (), s32[]{:S(2)}) async-start(), calls=%async_computation.4 | async-start | bytes 2097152 | tf_op jit(solution)/shard_map/psum | solution.py:32
  222.8 140.3 %all-reduce.15.cloned.1.call-start = ((), (), s32[]{:S(2)}) async-start(), calls=%async_computation.5 | async-start | bytes 1048576 | tf_op jit(solution)/shard_map/psum | solution.py:34
  272.2 114.8 %all-reduce.17.cloned.1.call-start = ((), (), s32[]{:S(2)}) async-start(), calls=%async_computation.6 | async-start | bytes 131072 | tf_op jit(solution)/shard_map/psum | solution.py:35
  365.5 80.4 %reduce-scatter.2.cloned.1.call-start = ((), (), s32[]{:S(2)}) async-start(), calls=%async_computation.7 | async-start | bytes 1572864 | tf_op jit(solution)/shard_map/reduce_scatter | solution.py:37
Sparse Core Ops, SparseCore 0:
  17.6 42.8 all-reduce.6
  69.7 90.6 all-reduce.8
  163.0 21.3 all-reduce.10
  222.9 40.0 all-reduce.12
  272.3 90.6 all-reduce.14
  365.6 21.3 all-reduce.16
  425.5 20.3 reduce-scatter.1
where the time goes:
time: 455 us
  waiting for transfers between devices  328 us (72%)
  matrix products  60.2 us (13%)
  other arithmetic  47.4 us (10%)
  between operations  13.6 us (3%)
  local copies, waits for them, and re-layouts  4.93 us (1%)
    psum x2, waiting for transfers between devices, on_device(): image = lax.psum(partial_value, 'cell')  182 us
    psum x2, waiting for transfers between devices, on_device(): spatial = lax.psum(local_terms, 'tm')  83.1 us
    psum x2, waiting for transfers between devices, on_device(): gram = lax.psum(tall_product(image, image), 'tm')  42.6 us
    another operation x6, other arithmetic, orthonormal(): lower = jnp.linalg.cholesky(gram)  24.8 us
    dot_general x4, matrix products, tall_product(): lax.dot_general(left, right, (((0,), (0,)), ((), ())), precision=lax.Prec...  23.1 us
    dot_general x2, matrix products, on_device(): jnp.dot(anomalies, current, precision=full, preferred_element_type=jnp.fl...  21.8 us
    another operation x4, other arithmetic, orthonormal(): return jax.scipy.linalg.solve_triangular(lower, image.T, lower=True).T  20.9 us
    reduce_scatter x1, waiting for transfers between devices, on_device(): lax.psum_scatter(jnp.dot(anomalies, basis, precision=full, preferred_elem...  20.5 us
  transfers between devices with their start and end apart: 7, of which 7 were waited for; matrix products, arithmetic and copies ran while one was open for 0% of the time, Pallas kernels for 0%

commit v1 on v0

v1 whole, which is shorter than its diff:
```python
import functools

import jax
import jax.numpy as jnp
from jax import lax
from jax.experimental import pallas as pl
from jax.experimental.pallas import tpu as pltpu
from jax.sharding import PartitionSpec as P

ITERS = 2
GROUPS = 2
CHUNKS = 4
PAIR = 2
SUB = 8
MESH = pl.DeviceIdType.MESH
NT = (((1,), (1,)), ((), ()))
NN = (((1,), (0,)), ((), ()))


def split(x):
    hi = x.astype(jnp.bfloat16)
    return hi, (x - hi.astype(jnp.float32)).astype(jnp.bfloat16)


def dot3(x, hi, lo, dims):
    rows = x.shape[0]
    x_hi, x_lo = split(x)
    both = lax.dot_general(
        jnp.concatenate([x_hi, x_lo], axis=0), hi, dims, preferred_element_type=jnp.float32
    )
    low = lax.dot_general(x_hi, lo, dims, preferred_element_type=jnp.float32)
    return both[:rows] + (both[rows:] + low)


def dot_full(x, y, dims):
    return lax.dot_general(
        x, y, dims, precision=lax.Precision.HIGHEST, preferred_element_type=jnp.float32
    )


def eliminate(mat, first, last):
    k = mat.shape[1]
    row = lax.broadcasted_iota(jnp.int32, (k, 1), 0)

    def body(step, carry):
        left, right = carry
        live = k - step * SUB
        for j in range(SUB):
            col = jnp.broadcast_to(left[:, j : j + 1], (k, k))
            inv = 1.0 / col[j : j + 1, :]
            factor = jnp.where((row > j) & (row < live), col, 0.0)
            l_row = left[j : j + 1, :] * inv
            r_row = right[j : j + 1, :] * inv
            left = left - factor * l_row
            right = right - factor * r_row
        diag = jnp.sum(
            jnp.where(
                lax.broadcasted_iota(jnp.int32, (SUB, k), 0)
                == lax.broadcasted_iota(jnp.int32, (SUB, k), 1),
                left[:SUB],
                0.0,
            ),
            axis=1,
            keepdims=True,
        )
        done = right[:SUB] * lax.rsqrt(diag)
        right = jnp.concatenate([right[SUB:], done], axis=0)
        left = jnp.concatenate([left[SUB:], left[:SUB]], axis=0)
        left = pltpu.roll(left, k - SUB, 1)
        return left, right

    left, right = lax.fori_loop(first, last, body, (mat[0], mat[1]))
    mat[0] = left
    mat[1] = right


def kernel(
    n_cell, n_tm, a_hbm, b_ref, out_ref,
    a_f32, a_hi, a_lo, send_s, recv_s, send_i, recv_a, half, recv_b, full, norm,
    gram_s, gram_r, mat1, mat2, send_p, recv_p, own_p,
    load_sem, s_ss, s_rs, a_ss, a_rs, b_ss, b_rs, c_ss, c_rs, d_ss, d_rs,
    g_ss, g_rs, p_ss, p_rs,
):
    cell, tm = lax.axis_index("cell"), lax.axis_index("tm")
    chip, core = cell // PAIR, cell % PAIR
    n_chip = n_cell // PAIR
    cells, hours = a_hbm.shape
    k = b_ref.shape[1]
    kg = k // GROUPS
    rows = cells // CHUNKS
    mid = hours // PAIR
    piece_rows = max(SUB, kg // n_chip)
    n_down = kg // piece_rows
    piece_cols = mid // (n_chip // n_down)
    part = cells // n_tm

    loads = []
    for c in range(CHUNKS):
        block = pl.ds(c * rows, rows)
        copy = pltpu.make_async_copy(a_hbm.at[block], a_f32.at[block], load_sem.at[c])
        copy.start()
        loads.append(copy)

    def tm_peer(d):
        return {"cell": cell, "tm": (tm + d) % n_tm}

    def chip_peer(d):
        return {"cell": ((chip + d) % n_chip) * PAIR + core, "tm": tm}

    sibling = {"cell": chip * PAIR + (1 - core), "tm": tm}
    peers = [tm_peer(d) for d in range(1, n_tm)]
    peers += [chip_peer(d) for d in range(1, n_chip)] + [sibling]
    barrier = pltpu.get_barrier_semaphore()
    for peer in peers:
        pl.semaphore_signal(barrier, inc=1, device_id=peer, device_id_type=MESH)
    pl.semaphore_wait(barrier, len(peers))

    started = {}

    def send(key, src, dst, ss, rs, peer):
        copy = pltpu.make_async_remote_copy(
            src_ref=src, dst_ref=dst, send_sem=ss, recv_sem=rs,
            device_id=peer, device_id_type=MESH,
        )
        copy.start()
        started[key] = copy

    def arrived(*key):
        started[key].wait_recv()

    def send_spatial(it, g, c):
        for d in range(1, n_tm):
            send(("s", it, g, c, d), send_s.at[it, g, c], recv_s.at[it, g, c, d - 1],
                 s_ss.at[it, g, c, d - 1], s_rs.at[it, g, c, d - 1], tm_peer(d))

    def chunk(it, g, c):
        for d in range(1, n_tm):
            arrived("s", it, g, c, d)
        spatial = send_s[it, g, c]
        for d in range(1, n_tm):
            spatial = spatial + recv_s[it, g, c, d - 1]
        block = pl.ds(c * rows, rows)
        term = dot3(spatial, a_hi[block, :], a_lo[block, :], NN)
        send_i[it, g] = term if c == 0 else send_i[it, g] + term

    mine = pl.ds(pl.multiple_of(core * mid, mid), mid)
    other = pl.ds(pl.multiple_of((1 - core) * mid, mid), mid)

    def place(q):
        down = pl.ds(pl.multiple_of((q % n_down) * piece_rows, piece_rows), piece_rows)
        return down, (q // n_down) * piece_cols

    def sum_pair(it, g):
        send(("a", it, g), send_i.at[it, g, :, other], recv_a.at[it, g],
             a_ss.at[it, g], a_rs.at[it, g], sibling)

    def sum_chips(it, g):
        arrived("a", it, g)
        half[it, g] = send_i[it, g, :, mine] + recv_a[it, g]
        for d in range(1, n_chip):
            down, across = place((chip + d) % n_chip)
            across = pl.ds(pl.multiple_of(across, piece_cols), piece_cols)
            send(("b", it, g, d), half.at[it, g, down, across], recv_b.at[it, g, d - 1],
                 b_ss.at[it, g, d - 1], b_rs.at[it, g, d - 1], chip_peer(d))

    def give_chips(it, g):
        down, across = place(chip)
        at_half = pl.ds(pl.multiple_of(across, piece_cols), piece_cols)
        at_full = pl.ds(pl.multiple_of(core * mid + across, piece_cols), piece_cols)
        total = half[it, g, down, at_half]
        for d in range(1, n_chip):
            arrived("b", it, g, d)
            total = total + recv_b[it, g, d - 1]
        full[it, g, down, at_full] = total
        for d in range(1, n_chip):
            spot = full.at[it, g, down, at_full]
            send(("c", it, g, d), spot, spot,
                 c_ss.at[it, g, d - 1], c_rs.at[it, g, d - 1], chip_peer(d))

    def give_pair(it, g):
        for d in range(1, n_chip):
            down, across = place((chip + n_chip - d) % n_chip)
            at_full = pl.ds(pl.multiple_of(core * mid + across, piece_cols), piece_cols)
            spot = full.at[it, g, down, at_full]
            pltpu.make_async_remote_copy(
                src_ref=spot, dst_ref=spot, send_sem=c_ss.at[it, g, d - 1],
                recv_sem=c_rs.at[it, g, d - 1], device_id=chip_peer(d), device_id_type=MESH,
            ).wait_recv()
        spot = full.at[it, g, :, mine]
        send(("d", it, g), spot, spot, d_ss.at[it, g], d_rs.at[it, g], sibling)

    def complete(it, g):
        spot = full.at[it, g, :, other]
        pltpu.make_async_remote_copy(
            src_ref=spot, dst_ref=spot, send_sem=d_ss.at[it, g], recv_sem=d_rs.at[it, g],
            device_id=sibling, device_id_type=MESH,
        ).wait_recv()

    def next_spatial(it, g):
        image = full[it - 1, g]
        for c in range(CHUNKS):
            block = pl.ds(c * rows, rows)
            send_s[it, g, c] = dot3(image, a_hi[block, :], a_lo[block, :], NT)
            send_spatial(it, g, c)

    def send_gram(it, blocks):
        image = jnp.concatenate(blocks, axis=0)
        gram_s[it] = dot_full(image, image, NT)
        for d in range(1, n_tm):
            send(("g", it, d), gram_s.at[it], gram_r.at[it, d - 1],
                 g_ss.at[it, d - 1], g_rs.at[it, d - 1], tm_peer(d))

    def take_gram(it, mat):
        gram = gram_s[it]
        for d in range(1, n_tm):
            arrived("g", it, d)
            gram = gram + gram_r[it, d - 1]
        mat[0] = gram
        mat[1] = (
            lax.broadcasted_iota(jnp.int32, (k, k), 0)
            == lax.broadcasted_iota(jnp.int32, (k, k), 1)
        ).astype(jnp.float32)

    def normalise(g):
        raw = jnp.concatenate([full[1, h] for h in range(g + 1)], axis=0)
        norm[g] = dot_full(mat1[1, g * kg : (g + 1) * kg, : (g + 1) * kg], raw, NN)

    def cells_of(owner):
        return pl.ds(pl.multiple_of(owner * part, part), part)

    def send_patterns(g):
        for d in range(1, n_tm):
            block = cells_of((tm + d) % n_tm)
            send_p[g, d - 1] = dot3(norm[g], a_hi[block, :], a_lo[block, :], NT)
            send(("p", g, d), send_p.at[g, d - 1], recv_p.at[g, d - 1],
                 p_ss.at[g, d - 1], p_rs.at[g, d - 1], tm_peer(d))

    def own_patterns(g):
        block = cells_of(tm)
        own_p[g] = dot3(norm[g], a_hi[block, :], a_lo[block, :], NT)

    steps = k // SUB

    def part_of(n):
        eliminate(mat1, n * steps // 4, (n + 1) * steps // 4)

    basis = b_ref[...].T
    for c in range(CHUNKS):
        loads[c].wait()
        block = pl.ds(c * rows, rows)
        hi, lo = split(a_f32[block, :])
        a_hi[block, :] = hi
        a_lo[block, :] = lo
        spatial = dot3(basis, hi, lo, NT)
        for g in range(GROUPS):
            send_s[0, g, c] = spatial[g * kg : (g + 1) * kg]
        send_spatial(0, 0, c)
    for c in range(CHUNKS):
        send_spatial(0, 1, c)

    for c in range(CHUNKS):
        chunk(0, 0, c)
    sum_pair(0, 0)
    chunk(0, 1, 0)
    sum_chips(0, 0)
    chunk(0, 1, 1)
    chunk(0, 1, 2)
    give_chips(0, 0)
    chunk(0, 1, 3)
    sum_pair(0, 1)
    give_pair(0, 0)
    sum_chips(0, 1)
    complete(0, 0)
    next_spatial(1, 0)
    give_chips(0, 1)
    chunk(1, 0, 0)
    chunk(1, 0, 1)
    give_pair(0, 1)
    chunk(1, 0, 2)
    complete(0, 1)
    send_gram(0, [full[0, g] for g in range(GROUPS)])
    next_spatial(1, 1)
    chunk(1, 0, 3)
    sum_pair(1, 0)
    take_gram(0, mat1)
    sum_chips(1, 0)
    part_of(0)
    chunk(1, 1, 0)
    part_of(1)
    chunk(1, 1, 1)
    give_chips(1, 0)
    part_of(2)
    chunk(1, 1, 2)
    give_pair(1, 0)
    part_of(3)
    chunk(1, 1, 3)
    sum_pair(1, 1)
    complete(1, 0)
    normalise(0)
    sum_chips(1, 1)
    send_patterns(0)
    own_patterns(0)
    give_chips(1, 1)
    give_pair(1, 1)
    complete(1, 1)
    normalise(1)
    send_gram(1, [norm[g] for g in range(GROUPS)])
    send_patterns(1)
    take_gram(1, mat2)
    eliminate(mat2, 0, steps)
    own_patterns(1)
    blocks = []
    for g in range(GROUPS):
        total = own_p[g]
        for d in range(1, n_tm):
            arrived("p", g, d)
            total = total + recv_p[g, d - 1]
        blocks.append(total)
    out_ref[...] = dot_full(mat2[1], jnp.concatenate(blocks, axis=0), NN).T
    for copy in started.values():
        copy.wait_send()


def on_device(n_cell, n_tm, anomalies, start_basis):
    cells, hours = anomalies.shape
    k = start_basis.shape[1]
    kg, rows, mid = k // GROUPS, cells // CHUNKS, hours // PAIR
    n_chip = n_cell // PAIR
    piece_rows = max(SUB, kg // n_chip)
    piece_cols = mid // (n_chip // (kg // piece_rows))
    part = cells // n_tm
    far, near = n_tm - 1, n_chip - 1
    f32, bf16 = jnp.float32, jnp.bfloat16
    dma = pltpu.SemaphoreType.DMA
    pair_sem = lambda *shape: [dma(shape), dma(shape)]
    return pl.pallas_call(
        functools.partial(kernel, n_cell, n_tm),
        out_shape=jax.ShapeDtypeStruct((part, k), f32),
        in_specs=[
            pl.BlockSpec(memory_space=pl.ANY),
            pl.BlockSpec(memory_space=pltpu.VMEM),
        ],
        out_specs=pl.BlockSpec(memory_space=pltpu.VMEM),
        scratch_shapes=[
            pltpu.VMEM((cells, hours), f32),
            pltpu.VMEM((cells, hours), bf16),
            pltpu.VMEM((cells, hours), bf16),
            pltpu.VMEM((ITERS, GROUPS, CHUNKS, kg, rows), f32),
            pltpu.VMEM((ITERS, GROUPS, CHUNKS, far, kg, rows), f32),
            pltpu.VMEM((ITERS, GROUPS, kg, hours), f32),
            pltpu.VMEM((ITERS, GROUPS, kg, mid), f32),
            pltpu.VMEM((ITERS, GROUPS, kg, mid), f32),
            pltpu.VMEM((ITERS, GROUPS, near, piece_rows, piece_cols), f32),
            pltpu.VMEM((ITERS, GROUPS, kg, hours), f32),
            pltpu.VMEM((GROUPS, kg, hours), f32),
            pltpu.VMEM((ITERS, k, k), f32),
            pltpu.VMEM((ITERS, far, k, k), f32),
            pltpu.VMEM((2, k, k), f32),
            pltpu.VMEM((2, k, k), f32),
            pltpu.VMEM((GROUPS, far, kg, part), f32),
            pltpu.VMEM((GROUPS, far, kg, part), f32),
            pltpu.VMEM((GROUPS, kg, part), f32),
            dma((CHUNKS,)),
            *pair_sem(ITERS, GROUPS, CHUNKS, far),
            *pair_sem(ITERS, GROUPS),
            *pair_sem(ITERS, GROUPS, near),
            *pair_sem(ITERS, GROUPS, near),
            *pair_sem(ITERS, GROUPS),
            *pair_sem(ITERS, far),
            *pair_sem(GROUPS, far),
        ],
        compiler_params=pltpu.CompilerParams(
            collective_id=0, has_side_effects=True, vmem_limit_bytes=60 * 1024 * 1024
        ),
    )(anomalies, start_basis)


def solution(mesh):
    in_specs = (P("cell", "tm"), P("tm", None))
    out_specs = P(("cell", "tm"), None)
    return jax.shard_map(
        functools.partial(on_device, mesh.shape["cell"], mesh.shape["tm"]),
        mesh=mesh, in_specs=in_specs, out_specs=out_specs, check_vma=False,
    )
```

time: 455 us -> 106 us (0.23)
  waiting for transfers between devices: 328 us -> 0 us
  Pallas kernels: 0 us -> 104 us
  matrix products: 60.2 us -> 0 us
  other arithmetic: 47.4 us -> 0 us
  between operations: 13.6 us -> 0.01 us
    psum x6 -> x0, waiting for transfers between devices: 307 us -> none  [the longest x2 182 us: on_device(): image = lax.psum(partial_value, 'cell')]
    pallas_call x0 -> x1, Pallas kernels: none -> 104 us  [on_device(): pl.pallas_call(functools.partial(kernel, n_cell, n_tm), out_shape=jax.Sha...]
    dot_general x7 -> x0, matrix products: 56.9 us -> none  [the longest x4 23.1 us: tall_product(): lax.dot_general(left, right, (((0,), (0,)), ((), ())), precision=lax.Prec...]
    another operation x10 -> x0, other arithmetic: 45.7 us -> none  [the longest x6 24.8 us: orthonormal(): lower = jnp.linalg.cholesky(gram)]
    reduce_scatter x1 -> x0, waiting for transfers between devices: 20.5 us -> none  [on_device(): lax.psum_scatter(jnp.dot(anomalies, basis, precision=full, preferred_elem...]
  transfers between devices with their start and end apart: 7 -> 0, of which waited for: 7 -> 0; matrix products, arithmetic and copies ran while one was open for 0% -> 0% of each run, Pallas kernels for 0% -> 0%
where the time goes in v1:
time: 106 us
  Pallas kernels  104 us (98%)
  local copies, waits for them, and re-layouts  1.87 us (2%)
    pallas_call x1, Pallas kernels, on_device(): pl.pallas_call(functools.partial(kernel, n_cell, n_tm), out_shape=jax.Sha...  104 us

profile of v1, /device:TPU:0, one launch (start us, length us, event | category | flops | bytes accessed | tf_op | source)
XLA Modules:
  0.0 106.0 jit_solution(5605887140873259555)
XLA Ops:
  0.0 104.1 %shard_map.28 = f32[1024,128]{1,0:T(8,128)} custom-call(f32[2048,1024]{1,0:T(8,128)} %a_hbm.1, f32[1024,128]{1,0:T(8,128)} %b_ref.1), custom_call_target="tpu_custom_call" | custom-call | tf_op jit(solution)/shard_map/pallas_call | solution.py:336
  104.1 1.9 %copy.4 = f32[1024,128]{1,0:T(8,128)} copy(f32[1024,128]{1,0:T(8,128)} %shard_map.28) | data formatting | bytes 1048576

commit v2 on v1

--- a/solution.py
+++ b/solution.py
@@ -38,46 +38,34 @@
     )
 
 
-def eliminate(mat, first, last):
-    k = mat.shape[1]
+def inverse_factor(gram):
+    k = gram.shape[0]
     row = lax.broadcasted_iota(jnp.int32, (k, 1), 0)
-
-    def body(step, carry):
-        left, right = carry
+    square = (k, k)
+    eye = lax.broadcasted_iota(jnp.int32, square, 0) == lax.broadcasted_iota(jnp.int32, square, 1)
+    corner = (SUB, 2 * k)
+    diagonal = lax.broadcasted_iota(jnp.int32, corner, 0) == lax.broadcasted_iota(
+        jnp.int32, corner, 1
+    )
+
+    def body(step, both):
         live = k - step * SUB
         for j in range(SUB):
-            col = jnp.broadcast_to(left[:, j : j + 1], (k, k))
-            inv = 1.0 / col[j : j + 1, :]
-            factor = jnp.where((row > j) & (row < live), col, 0.0)
-            l_row = left[j : j + 1, :] * inv
-            r_row = right[j : j + 1, :] * inv
-            left = left - factor * l_row
-            right = right - factor * r_row
-        diag = jnp.sum(
-            jnp.where(
-                lax.broadcasted_iota(jnp.int32, (SUB, k), 0)
-                == lax.broadcasted_iota(jnp.int32, (SUB, k), 1),
-                left[:SUB],
-                0.0,
-            ),
-            axis=1,
-            keepdims=True,
-        )
-        done = right[:SUB] * lax.rsqrt(diag)
-        right = jnp.concatenate([right[SUB:], done], axis=0)
-        left = jnp.concatenate([left[SUB:], left[:SUB]], axis=0)
-        left = pltpu.roll(left, k - SUB, 1)
-        return left, right
-
-    left, right = lax.fori_loop(first, last, body, (mat[0], mat[1]))
-    mat[0] = left
-    mat[1] = right
+            col = jnp.broadcast_to(both[:, j : j + 1], (k, 2 * k))
+            scaled = both[j : j + 1, :] * (1.0 / col[j : j + 1, :])
+            both = both - jnp.where((row > j) & (row < live), col, 0.0) * scaled
+        pivots = jnp.sum(jnp.where(diagonal, both[:SUB], 0.0), axis=1, keepdims=True)
+        done = both[:SUB] * lax.rsqrt(pivots)
+        return pltpu.roll(jnp.concatenate([both[SUB:], done], axis=0), 2 * k - SUB, 1)
+
+    start = jnp.concatenate([gram, eye.astype(jnp.float32)], axis=1)
+    return lax.fori_loop(0, k // SUB, body, start)[:, :k]
 
 
 def kernel(
     n_cell, n_tm, a_hbm, b_ref, out_ref,
     a_f32, a_hi, a_lo, send_s, recv_s, send_i, recv_a, half, recv_b, full, norm,
-    gram_s, gram_r, mat1, mat2, send_p, recv_p, own_p,
+    gram_s, gram_r, lin, send_p, recv_p, own_p,
     load_sem, s_ss, s_rs, a_ss, a_rs, b_ss, b_rs, c_ss, c_rs, d_ss, d_rs,
     g_ss, g_rs, p_ss, p_rs,
 ):
@@ -203,27 +191,30 @@
             send_s[it, g, c] = dot3(image, a_hi[block, :], a_lo[block, :], NT)
             send_spatial(it, g, c)
 
-    def send_gram(it, blocks):
-        image = jnp.concatenate(blocks, axis=0)
-        gram_s[it] = dot_full(image, image, NT)
-        for d in range(1, n_tm):
-            send(("g", it, d), gram_s.at[it], gram_r.at[it, d - 1],
-                 g_ss.at[it, d - 1], g_rs.at[it, d - 1], tm_peer(d))
-
-    def take_gram(it, mat):
-        gram = gram_s[it]
-        for d in range(1, n_tm):
-            arrived("g", it, d)
-            gram = gram + gram_r[it, d - 1]
-        mat[0] = gram
-        mat[1] = (
-            lax.broadcasted_iota(jnp.int32, (k, k), 0)
-            == lax.broadcasted_iota(jnp.int32, (k, k), 1)
-        ).astype(jnp.float32)
+    def send_gram(it, g, blocks):
+        gram_s[it, g] = dot_full(blocks[g], jnp.concatenate(blocks, axis=0), NT)
+        for d in range(1, n_tm):
+            send(("g", it, g, d), gram_s.at[it, g], gram_r.at[it, g, d - 1],
+                 g_ss.at[it, g, d - 1], g_rs.at[it, g, d - 1], tm_peer(d))
+
+    def factor(it, g):
+        gram = gram_s[it, g]
+        for d in range(1, n_tm):
+            arrived("g", it, g, d)
+            gram = gram + gram_r[it, g, d - 1]
+        if g == 0:
+            inv = inverse_factor(gram[:, :kg])
+            lin[it, 0] = jnp.concatenate([inv, jnp.zeros_like(inv)], axis=1)
+        else:
+            first = lin[it, 0, :, :kg]
+            below = dot_full(gram[:, :kg], first, NT)
+            inv = inverse_factor(gram[:, kg:] - dot_full(below, below, NT))
+            left = dot_full(dot_full(inv, below, NN), first, NN)
+            lin[it, 1] = jnp.concatenate([-left, inv], axis=1)
 
     def normalise(g):
         raw = jnp.concatenate([full[1, h] for h in range(g + 1)], axis=0)
-        norm[g] = dot_full(mat1[1, g * kg : (g + 1) * kg, : (g + 1) * kg], raw, NN)
+        norm[g] = dot_full(lin[0, g, :, : (g + 1) * kg], raw, NN)
 
     def cells_of(owner):
         return pl.ds(pl.multiple_of(owner * part, part), part)
@@ -238,11 +229,6 @@
     def own_patterns(g):
         block = cells_of(tm)
         own_p[g] = dot3(norm[g], a_hi[block, :], a_lo[block, :], NT)
-
-    steps = k // SUB
-
-    def part_of(n):
-        eliminate(mat1, n * steps // 4, (n + 1) * steps // 4)
 
     basis = b_ref[...].T
     for c in range(CHUNKS):
@@ -261,11 +247,11 @@
     for c in range(CHUNKS):
         chunk(0, 0, c)
     sum_pair(0, 0)
+    sum_chips(0, 0)
     chunk(0, 1, 0)
-    sum_chips(0, 0)
     chunk(0, 1, 1)
+    give_chips(0, 0)
     chunk(0, 1, 2)
-    give_chips(0, 0)
     chunk(0, 1, 3)
     sum_pair(0, 1)
     give_pair(0, 0)
@@ -273,41 +259,40 @@
     complete(0, 0)
     next_spatial(1, 0)
     give_chips(0, 1)
+    send_gram(0, 0, [full[0, 0], full[0, 0]])
+    give_pair(0, 1)
     chunk(1, 0, 0)
+    complete(0, 1)
+    next_spatial(1, 1)
     chunk(1, 0, 1)
-    give_pair(0, 1)
+    send_gram(0, 1, [full[0, 0], full[0, 1]])
     chunk(1, 0, 2)
-    complete(0, 1)
-    send_gram(0, [full[0, g] for g in range(GROUPS)])
-    next_spatial(1, 1)
     chunk(1, 0, 3)
     sum_pair(1, 0)
-    take_gram(0, mat1)
     sum_chips(1, 0)
-    part_of(0)
+    factor(0, 0)
     chunk(1, 1, 0)
-    part_of(1)
     chunk(1, 1, 1)
+    chunk(1, 1, 2)
     give_chips(1, 0)
-    part_of(2)
-    chunk(1, 1, 2)
-    give_pair(1, 0)
-    part_of(3)
     chunk(1, 1, 3)
     sum_pair(1, 1)
+    give_pair(1, 0)
+    sum_chips(1, 1)
     complete(1, 0)
     normalise(0)
-    sum_chips(1, 1)
     send_patterns(0)
+    send_gram(1, 0, [norm[0], norm[0]])
+    factor(0, 1)
+    give_chips(1, 1)
+    factor(1, 0)
+    give_pair(1, 1)
     own_patterns(0)
-    give_chips(1, 1)
-    give_pair(1, 1)
     complete(1, 1)
     normalise(1)
-    send_gram(1, [norm[g] for g in range(GROUPS)])
+    send_gram(1, 1, [norm[0], norm[1]])
     send_patterns(1)
-    take_gram(1, mat2)
-    eliminate(mat2, 0, steps)
+    factor(1, 1)
     own_patterns(1)
     blocks = []
     for g in range(GROUPS):
@@ -316,7 +301,10 @@
             arrived("p", g, d)
             total = total + recv_p[g, d - 1]
         blocks.append(total)
-    out_ref[...] = dot_full(mat2[1], jnp.concatenate(blocks, axis=0), NN).T
+    out_ref[...] = dot_full(
+        jnp.concatenate([lin[1, g] for g in range(GROUPS)], axis=0),
+        jnp.concatenate(blocks, axis=0), NN,
+    ).T
     for copy in started.values():
         copy.wait_send()
 
@@ -353,10 +341,9 @@
             pltpu.VMEM((ITERS, GROUPS, near, piece_rows, piece_cols), f32),
             pltpu.VMEM((ITERS, GROUPS, kg, hours), f32),
             pltpu.VMEM((GROUPS, kg, hours), f32),
-            pltpu.VMEM((ITERS, k, k), f32),
-            pltpu.VMEM((ITERS, far, k, k), f32),
-            pltpu.VMEM((2, k, k), f32),
-            pltpu.VMEM((2, k, k), f32),
+            pltpu.VMEM((ITERS, GROUPS, kg, k), f32),
+            pltpu.VMEM((ITERS, GROUPS, far, kg, k), f32),
+            pltpu.VMEM((ITERS, GROUPS, kg, k), f32),
             pltpu.VMEM((GROUPS, far, kg, part), f32),
             pltpu.VMEM((GROUPS, far, kg, part), f32),
             pltpu.VMEM((GROUPS, kg, part), f32),
@@ -366,7 +353,7 @@
             *pair_sem(ITERS, GROUPS, near),
             *pair_sem(ITERS, GROUPS, near),
             *pair_sem(ITERS, GROUPS),
-            *pair_sem(ITERS, far),
+            *pair_sem(ITERS, GROUPS, far),
             *pair_sem(GROUPS, far),
         ],
         compiler_params=pltpu.CompilerParams(

time: 106 us -> 101 us (0.953)
  Pallas kernels: 104 us -> 99 us
    pallas_call x1, Pallas kernels: 104 us -> 99 us  [on_device(): pl.pallas_call(functools.partial(kernel, n_cell, n_tm), out_shape=jax.Sha...]
where the time goes in v2:
time: 101 us
  Pallas kernels  99 us (98%)
  local copies, waits for them, and re-layouts  1.87 us (2%)
    pallas_call x1, Pallas kernels, on_device(): pl.pallas_call(functools.partial(kernel, n_cell, n_tm), out_shape=jax.Sha...  99 us

profile of v2, /device:TPU:0, one launch (start us, length us, event | category | flops | bytes accessed | tf_op | source)
XLA Modules:
  0.0 100.8 jit_solution(6599029609613593152)
XLA Ops:
  0.0 99.0 %shard_map.28 = f32[1024,128]{1,0:T(8,128)} custom-call(f32[2048,1024]{1,0:T(8,128)} %a_hbm.1, f32[1024,128]{1,0:T(8,128)} %b_ref.1), custom_call_target="tpu_custom_call" | custom-call | tf_op jit(solution)/shard_map/pallas_call | solution.py:324
  99.0 1.9 %copy.4 = f32[1024,128]{1,0:T(8,128)} copy(f32[1024,128]{1,0:T(8,128)} %shard_map.28) | data formatting | bytes 1048576
